TPU v7x, 128 devices: a whole 4x4x4 slice. The times are simulated.
128 devices in a mesh: row: 8 (over x, core), col: 16 (over z, y).
Axes of the slice: x: 4, y: 4, z: 4, core: 2. Of those that a mesh axis runs over, the one named last changes fastest.
Arguments:
- kernel: bfloat16 [32768, 32768], P('row', 'col'), may hold values from -1 to 1
- random_cols: bfloat16 [32768, 256], P('row'), may hold values from -6 to 6
- tree_perm: int32 [32768], replicated, may hold values from 0 to 32767, as said below
- leaf_units: int32 [32], replicated, may hold values from 1 to 8, 160 in all
Outputs:
- bases: bfloat16 [4, 32768, 256], P(None, ('row', 'col'))
Inputs may be any that keep to these rules, and one draw needn't show every extreme that they name: `tree_perm`: A permutation. Cut tree positions and stored rows alike into blocks of 256 in order: every tree block takes at most 2 rows from any one stored block, some pair of blocks shares exactly 2, and every stored block gives 256 rows in all. `leaf_units`: they sum to 160.
All inputs are finite; a program needn't handle non-finite values.
Results may differ from a plain program's by a relative error of at most 0.0067.
Values may be sent and summed in bfloat16 or wider, within the bound.
No kernel may reach another device: no remote copies, remote signals or barrier semaphores. Data moves between devices by JAX's collectives and lax.ppermute only.
A program may use at most 192 MiB of HBM per device.

v0:
```python
import jax
import jax.numpy as jnp
from jax import lax
from jax.sharding import PartitionSpec as P

UNIT = 128
MINU = 4
LEVELS = 3


def shards(kernel, random_cols, tree_perm, leaf_units):
    width = random_cols.shape[1]
    partial_w = lax.dot_general(
        kernel, random_cols, (((0,), (0,)), ((), ())), preferred_element_type=jnp.float32
    )
    sample_w = lax.psum(partial_w, "row").astype(jnp.bfloat16)
    columns_count = lax.axis_size("col")
    rows_dev = kernel.shape[0] // columns_count
    sample = lax.psum_scatter(
        jnp.dot(kernel, sample_w, preferred_element_type=jnp.float32),
        "col",
        scatter_dimension=0,
        tiled=True,
    ).astype(jnp.bfloat16)
    total_rows = tree_perm.shape[0]
    device = lax.axis_index(("row", "col"))
    offset = device * rows_dev
    wanted = lax.dynamic_slice_in_dim(tree_perm, offset, rows_dev)
    inverse = (
        jnp.zeros((total_rows,), jnp.int32)
        .at[tree_perm]
        .set(jnp.arange(total_rows, dtype=jnp.int32))
    )
    placed = lax.dynamic_slice_in_dim(inverse, offset, rows_dev)
    everything = lax.all_gather(sample, ("row", "col"), axis=0, tiled=True)
    tree_rows = jnp.take(everything, wanted, axis=0)
    sizes = UNIT * (MINU - 1 + leaf_units)
    leaves = sizes.shape[0]
    ends = jnp.cumsum(sizes)
    positions = offset + jnp.arange(rows_dev, dtype=jnp.int32)
    leaf_of = jnp.sum(positions[:, None] >= ends[None, :], axis=1)
    reach = rows_dev // (UNIT * MINU) + 2
    offsets = jnp.arange(reach, dtype=jnp.int32)
    levels = LEVELS + 1
    node_ids = [leaf_of // 2**level for level in range(levels)]
    totals = []
    stored_leaf = jnp.sum(placed[:, None] >= ends[None, :], axis=1)
    leaf_range = jnp.arange(leaves, dtype=jnp.int32)
    chosen = stored_leaf[None, :] == leaf_range[:, None]
    masked = jnp.where(chosen[:, :, None], sample[None, :, :], jnp.zeros((), jnp.bfloat16))
    spread = jnp.einsum("lrs,rt->lst", masked, sample, preferred_element_type=jnp.float32)
    leaf_grams = lax.psum(spread, ("row", "col"))
    for level in range(levels):
        group = 2**level
        count = leaves // group
        node_grams = leaf_grams.reshape(count, group, width, width).sum(axis=1)
        index = jnp.minimum(node_ids[level][0] + offsets, count - 1)
        totals.append(jnp.take(node_grams, index, axis=0))
    identity_matrix = jnp.eye(width, dtype=jnp.float32)
    values = tree_rows.astype(jnp.float32).T
    results = []
    for level in range(levels):
        ids = node_ids[level]
        group = 2**level
        count = leaves // group
        node_sizes = sizes.reshape(count, group).sum(axis=1)
        candidate = ids[0] + offsets
        present = candidate <= ids[-1]
        counts = jnp.take(node_sizes, jnp.minimum(candidate, count - 1)).astype(jnp.float32)
        mean = jnp.where(
            present[:, None, None], totals[level] / counts[:, None, None], identity_matrix[None]
        )
        factor = jnp.linalg.cholesky(mean)
        basis = jnp.zeros((rows_dev, width), jnp.float32)
        for which in range(reach):
            solved = jax.scipy.linalg.solve_triangular(factor[which], values, lower=True).T
            basis = basis + jnp.where((ids == candidate[which])[:, None], solved, 0.0)
        results.append(basis.astype(jnp.bfloat16))
    return jnp.stack(results)


def solution(mesh):
    return jax.shard_map(
        shards,
        mesh=mesh,
        in_specs=(P("row", "col"), P("row", None), P(), P()),
        out_specs=P(None, ("row", "col"), None),
        check_vma=False,
    )
```

profile of v0, /device:TPU:1, one launch (start us, length us, event | category | flops | bytes accessed | tf_op | source)
XLA Modules:
  0.0 931.9 jit_solution(916774655061557949)
XLA Ops:
  8.1 9.7 %fusion.100 = f32[2048,256]{1,0:T(8,128)} fusion(bf16[4096,2048]{1,0:T(8,128)(2,1)} %param.7, bf16[4096,256]{1,0:T(8,128)(2,1)S(1)} %copy-done), kind=kOutput, calls=%fused_computation.278 | convolution fusion | flops 4294967296 | bytes 20971520 | tf_op jit(solution)/shard_map/dot_general | solution.py:13
  17.8 52.9 %all-reduce.5 = bf16[2048,256]{1,0:T(8,128)(2,1)S(1)} all-reduce(f32[2048,256]{1,0:T(8,128)} %fusion.100), channel_id=1, replica_groups=mesh['row'=8,'col'=16] {'row'}, use_global_device_ids=true, to_apply=%region_4.5 | all-reduce | flops 524288 | bytes 3145728 | tf_op jit(solution)/shard_map/psum | solution.py:16
  70.7 10.1 %convolution_bitcast_fusion = f32[4096,256]{0,1:T(8,128)} fusion(bf16[4096,2048]{1,0:T(8,128)(2,1)} %param.7, bf16[2048,256]{1,0:T(8,128)(2,1)S(1)} %all-reduce.5), kind=kOutput, calls=%fused_computation.29 | convolution fusion | flops 4294967296 | bytes 22020096 | tf_op jit(solution)/shard_map/dot_general | solution.py:20
  81.9 120.1 %scatter_custom_fusion = s32[32768]{0:T(1024)S(1)} fusion(s32[32768]{0:T(1024)S(1)} %compare_select_fusion, s32[32768]{0:T(1024)S(1)} %iota.117, s32[]{:T(128)} %copy.139), kind=kCustom, calls=%fused_computation.181 | custom fusion | bytes 131076 | tf_op jit(solution)/shard_map/scatter | solution.py:32
  203.1 4.5 fusion
  207.7 12.0 %all-gather.2.cloned.1.call-start = ((), (), s32[]{:S(2)}) async-start(), calls=%async_computation.3 | async-start | bytes 16908288 | tf_op jit(solution)/shard_map/all_gather | solution.py:35
  253.2 119.0 %all-reduce.4.cloned.1.call-done = f32[32,256,256]{2,1,0:T(8,128)} async-done(((f32[32,256,256]{2,1,0:T(8,128)}), f32[32,256,256]{2,1,0:T(8,128)}) %all-reduce.4.cloned.1.call-update) | async-done | bytes 8388624 | tf_op jit(solution)/shard_map/psum | solution.py:52
  372.1 4.2 bitcast_reduce_fusion.1
  377.2 6.5 bitcast_reduce_fusion.2
  400.0 23.5 %custom-call.29 = f32[2,128,128]{2,1,0:T(8,128)S(1)} custom-call(f32[2,128,128]{2,1,0:T(8,128)S(1)} %cholesky.350), custom_call_target="Cholesky" | custom-call | tf_op jit(solution)/shard_map/jit(cholesky)/cholesky | solution.py:73
  423.7 23.5 %custom-call.39 = f32[2,128,128]{2,1,0:T(8,128)S(1)} custom-call(f32[2,128,128]{2,1,0:T(8,128)S(1)} %cholesky.356), custom_call_target="Cholesky" | custom-call | tf_op jit(solution)/shard_map/jit(cholesky)/cholesky | solution.py:73
  448.3 23.5 %custom-call.34 = f32[2,128,128]{2,1,0:T(8,128)S(1)} custom-call(f32[2,128,128]{2,1,0:T(8,128)S(1)} %cholesky.353), custom_call_target="Cholesky" | custom-call | tf_op jit(solution)/shard_map/jit(cholesky)/cholesky | solution.py:73
  472.1 23.9 %custom-call.44 = f32[2,128,128]{2,1,0:T(8,128)S(1)} custom-call(f32[2,128,128]{2,1,0:T(8,128)S(1)} %cholesky.359), custom_call_target="Cholesky" | custom-call | tf_op jit(solution)/shard_map/jit(cholesky)/cholesky | solution.py:73
  497.4 19.7 %custom-call.30 = f32[2,1,128,128]{2,3,1,0:T(8,128)S(1)} custom-call(f32[2,1,128,128]{3,2,1,0:T(8,128)S(1)} %get-tuple-element.180), custom_call_target="InvertDiagBlocksLowerTriangular" | custom-call | tf_op jit(solution)/shard_map/jit(cholesky)/cholesky | solution.py:73
  517.8 23.5 %custom-call.31 = f32[2,128,128]{2,1,0:T(8,128)S(1)} custom-call(f32[2,128,128]{2,1,0:T(8,128)S(1)} %convolution_subtract_fusion.11), custom_call_target="Cholesky" | custom-call | tf_op jit(solution)/shard_map/jit(cholesky)/cholesky | solution.py:73
  541.3 19.8 %custom-call.35 = f32[2,1,128,128]{2,3,1,0:T(8,128)S(1)} custom-call(f32[2,1,128,128]{3,2,1,0:T(8,128)S(1)} %get-tuple-element.178), custom_call_target="InvertDiagBlocksLowerTriangular" | custom-call | tf_op jit(solution)/shard_map/jit(cholesky)/cholesky | solution.py:73
  563.7 23.5 %custom-call.36 = f32[2,128,128]{2,1,0:T(8,128)S(1)} custom-call(f32[2,128,128]{2,1,0:T(8,128)S(1)} %convolution_subtract_fusion.10), custom_call_target="Cholesky" | custom-call | tf_op jit(solution)/shard_map/jit(cholesky)/cholesky | solution.py:73
  587.2 21.1 %custom-call.40 = f32[2,1,128,128]{2,3,1,0:T(8,128)} custom-call(f32[2,1,128,128]{3,2,1,0:T(8,128)} %get-tuple-element.177), custom_call_target="InvertDiagBlocksLowerTriangular" | custom-call | tf_op jit(solution)/shard_map/jit(cholesky)/cholesky | solution.py:73
  610.5 25.1 %custom-call.41 = f32[2,128,128]{2,1,0:T(8,128)} custom-call(f32[2,128,128]{2,1,0:T(8,128)} %convolution_subtract_fusion.9), custom_call_target="Cholesky" | custom-call | tf_op jit(solution)/shard_map/jit(cholesky)/cholesky | solution.py:73
  636.5 21.1 %custom-call.45 = f32[2,1,128,128]{2,3,1,0:T(8,128)} custom-call(f32[2,1,128,128]{3,2,1,0:T(8,128)} %get-tuple-element.179), custom_call_target="InvertDiagBlocksLowerTriangular" | custom-call | tf_op jit(solution)/shard_map/jit(cholesky)/cholesky | solution.py:73
  659.9 24.3 %custom-call.46 = f32[2,128,128]{2,1,0:T(8,128)S(1)} custom-call(f32[2,128,128]{2,1,0:T(8,128)} %convolution_subtract_fusion.8), custom_call_target="Cholesky" | custom-call | tf_op jit(solution)/shard_map/jit(cholesky)/cholesky | solution.py:73
  692.3 20.1 %custom-call.48 = f32[2,128,128]{1,2,0:T(8,128)S(1)} custom-call(f32[2,128,128]{2,1,0:T(8,128)S(1)} %get-tuple-element.64), custom_call_target="InvertDiagBlocksLowerTriangular" | custom-call | tf_op jit(solution)/shard_map/jit(_solve_triangular)/triangular_solve | solution.py:76
  716.4 20.3 %custom-call.47 = f32[2,128,128]{1,2,0:T(8,128)} custom-call(f32[2,128,128]{2,1,0:T(8,128)S(1)} %get-tuple-element.63), custom_call_target="InvertDiagBlocksLowerTriangular" | custom-call | tf_op jit(solution)/shard_map/jit(_solve_triangular)/triangular_solve | solution.py:76
  736.7 4.1 while.21
  740.8 19.7 %custom-call.43 = f32[2,128,128]{1,2,0:T(8,128)S(1)} custom-call(f32[2,128,128]{2,1,0:T(8,128)S(1)} %get-tuple-element.62), custom_call_target="InvertDiagBlocksLowerTriangular" | custom-call | tf_op jit(solution)/shard_map/jit(_solve_triangular)/triangular_solve | solution.py:76
  764.5 19.7 %custom-call.42 = f32[2,128,128]{1,2,0:T(8,128)S(1)} custom-call(f32[2,128,128]{2,1,0:T(8,128)S(1)} %get-tuple-element.61), custom_call_target="InvertDiagBlocksLowerTriangular" | custom-call | tf_op jit(solution)/shard_map/jit(_solve_triangular)/triangular_solve | solution.py:76
  788.1 19.7 %custom-call.38 = f32[2,128,128]{1,2,0:T(8,128)S(1)} custom-call(f32[2,128,128]{2,1,0:T(8,128)S(1)} %get-tuple-element.60), custom_call_target="InvertDiagBlocksLowerTriangular" | custom-call | tf_op jit(solution)/shard_map/jit(_solve_triangular)/triangular_solve | solution.py:76
  811.7 20.5 %custom-call.37 = f32[2,128,128]{1,2,0:T(8,128)} custom-call(f32[2,128,128]{2,1,0:T(8,128)S(1)} %get-tuple-element.59), custom_call_target="InvertDiagBlocksLowerTriangular" | custom-call | tf_op jit(solution)/shard_map/jit(_solve_triangular)/triangular_solve | solution.py:76
  836.1 20.3 %custom-call.33 = f32[2,128,128]{1,2,0:T(8,128)} custom-call(f32[2,128,128]{2,1,0:T(8,128)S(1)} %get-tuple-element.58), custom_call_target="InvertDiagBlocksLowerTriangular" | custom-call | tf_op jit(solution)/shard_map/jit(_solve_triangular)/triangular_solve | solution.py:76
  860.0 20.3 %custom-call.32 = f32[2,128,128]{1,2,0:T(8,128)} custom-call(f32[2,128,128]{2,1,0:T(8,128)S(1)} %get-tuple-element.57), custom_call_target="InvertDiagBlocksLowerTriangular" | custom-call | tf_op jit(solution)/shard_map/jit(_solve_triangular)/triangular_solve | solution.py:76
  880.3 22.6 %copy.47 = bf16[32768,256]{1,0:T(8,128)(2,1)} copy(bf16[32768,256]{0,1:T(8,128)(2,1)} %all-gather.2.cloned.1.call-done) | data formatting | bytes 33554432 | tf_op jit(solution)/shard_map/all_gather | solution.py:35
  902.9 9.0 gather_fusion.2
  (266 shorter events, 140.6 us)
Async XLA Ops:
  6.5 1.6 copy-start
  6.5 195.6 %reduce-scatter.2.cloned.1.call-start = ((), (), s32[]{:S(2)}) async-start(), calls=%async_computation.1 | async-start | bytes 4456448 | tf_op jit(solution)/shard_map/reduce_scatter | solution.py:19
  80.9 0.7 copy-start.25
  80.9 0.9 copy-start.11
  80.9 291.2 %all-reduce.4.cloned.1.call-start = ((), (), s32[]{:S(2)}) async-start(), calls=%async_computation.2 | async-start | bytes 16777216 | tf_op jit(solution)/shard_map/psum | solution.py:52
  203.1 4.5 copy-start.2
  207.7 672.6 %all-gather.2.cloned.1.call-start = ((), (), s32[]{:S(2)}) async-start(), calls=%async_computation.3 | async-start | bytes 16908288 | tf_op jit(solution)/shard_map/all_gather | solution.py:35
  399.2 0.8 copy-start.6
  423.7 93.4 %copy-start.7 = (f32[2,256,256]{2,1,0:T(8,128)S(1)}, f32[2,256,256]{2,1,0:T(8,128)}, u32[]{:S(2)}) copy-start(f32[2,256,256]{2,1,0:T(8,128)} %copy-done.6) | copy-start | bytes 1572868
  447.5 0.8 copy-start.8
  495.9 1.5 copy-start.9
  517.8 166.3 %copy-start.10 = (f32[2,128,128]{2,1,0:T(8,128)S(1)}, f32[2,128,128]{2,1,0:T(8,128)}, u32[]{:S(2)}) copy-start(f32[2,128,128]{2,1,0:T(8,128)} %copy-done.9) | copy-start | bytes 393220
  685.1 1.0 copy-start.3
  685.2 1.0 copy-start.4
  807.8 108.1 %copy-start.13 = (f32[2,128,128]{1,2,0:T(8,128)}, f32[2,128,128]{1,2,0:T(8,128)S(1)}, u32[]{:S(2)}) copy-start(f32[2,128,128]{1,2,0:T(8,128)S(1)} %custom-call.38) | copy-start | bytes 393220
  836.1 66.9 %copy-start.5 = (f32[256,256]{1,0:T(8,128)}, f32[256,256]{1,0:T(8,128)S(1)}, u32[]{:S(2)}) copy-start(f32[256,256]{1,0:T(8,128)S(1)} %get-tuple-element.602) | copy-start | bytes 786436
  880.3 31.8 %copy-start.24 = (pred[256]{0:T(512)(128)(4,1)S(1)}, pred[256]{0:T(512)(128)(4,1)}, u32[]{:S(2)}) copy-start(pred[256]{0:T(512)(128)(4,1)} %get-tuple-element.139) | copy-start | bytes 772
  880.3 32.8 %copy-start.12 = (f32[2,128,128]{1,2,0:T(8,128)S(1)}, f32[2,128,128]{1,2,0:T(8,128)}, u32[]{:S(2)}) copy-start(f32[2,128,128]{1,2,0:T(8,128)} %custom-call.47) | copy-start | bytes 393220
  912.1 10.5 %copy-start.14 = (f32[2,128,128]{1,2,0:T(8,128)S(1)}, f32[2,128,128]{1,2,0:T(8,128)}, u32[]{:S(2)}) copy-start(f32[2,128,128]{1,2,0:T(8,128)} %custom-call.33) | copy-start | bytes 393220
  912.1 10.8 %copy-start.15 = (f32[2,128,128]{1,2,0:T(8,128)S(1)}, f32[2,128,128]{1,2,0:T(8,128)}, u32[]{:S(2)}) copy-start(f32[2,128,128]{1,2,0:T(8,128)} %custom-call.32) | copy-start | bytes 393220
  912.4 11.4 %copy-start.18 = (pred[256]{0:T(512)(128)(4,1)S(1)}, pred[256]{0:T(512)(128)(4,1)}, u32[]{:S(2)}) copy-start(pred[256]{0:T(512)(128)(4,1)} %get-tuple-element.187) | copy-start | bytes 772
  912.5 11.4 %copy-start.19 = (pred[256]{0:T(512)(128)(4,1)S(1)}, pred[256]{0:T(512)(128)(4,1)}, u32[]{:S(2)}) copy-start(pred[256]{0:T(512)(128)(4,1)} %get-tuple-element.188) | copy-start | bytes 772
  913.1 10.8 %copy-start.16 = (pred[256]{0:T(512)(128)(4,1)S(1)}, pred[256]{0:T(512)(128)(4,1)}, u32[]{:S(2)}) copy-start(pred[256]{0:T(512)(128)(4,1)} %get-tuple-element.226) | copy-start | bytes 772
  913.1 10.8 %copy-start.17 = (pred[256]{0:T(512)(128)(4,1)S(1)}, pred[256]{0:T(512)(128)(4,1)}, u32[]{:S(2)}) copy-start(pred[256]{0:T(512)(128)(4,1)} %get-tuple-element.227) | copy-start | bytes 772
  913.7 10.3 %copy-start.22 = (pred[256]{0:T(512)(128)(4,1)S(1)}, pred[256]{0:T(512)(128)(4,1)}, u32[]{:S(2)}) copy-start(pred[256]{0:T(512)(128)(4,1)} %get-tuple-element.183) | copy-start | bytes 772
  913.7 10.3 %copy-start.23 = (pred[256]{0:T(512)(128)(4,1)S(1)}, pred[256]{0:T(512)(128)(4,1)}, u32[]{:S(2)}) copy-start(pred[256]{0:T(512)(128)(4,1)} %get-tuple-element.184) | copy-start | bytes 772
  914.3 9.7 %copy-start.20 = (pred[256]{0:T(512)(128)(4,1)S(1)}, pred[256]{0:T(512)(128)(4,1)}, u32[]{:S(2)}) copy-start(pred[256]{0:T(512)(128)(4,1)} %get-tuple-element.181) | copy-start | bytes 772
  914.3 9.7 %copy-start.21 = (pred[256]{0:T(512)(128)(4,1)S(1)}, pred[256]{0:T(512)(128)(4,1)}, u32[]{:S(2)}) copy-start(pred[256]{0:T(512)(128)(4,1)} %get-tuple-element.182) | copy-start | bytes 772
  916.2 9.0 copy-start.1
Sparse Core Ops, SparseCore 0:
  81.0 79.6 reduce-scatter.1
  207.8 164.3 all-reduce.3
  375.0 98.1 all-gather.1
where the time goes:
time: 940 us; the launch traced here: 932 us
  other arithmetic  481 us (51%)
  local copies, waits for them, and re-layouts  208 us (22%)
  waiting for transfers between devices  119 us (13%)
  blocking collectives  52.9 us (6%)
  matrix products  43.3 us (5%)
  between operations  14.6 us (2%)
  starting transfers between devices  12 us (1%)
    another operation x28, other arithmetic, shards(): factor = jnp.linalg.cholesky(mean)  276 us
    another operation x14, other arithmetic, shards(): jax.scipy.linalg.solve_triangular(factor[which], values, lower=True)  162 us
    scatter x1, local copies, waits for them, and re-layouts, shards(): inverse = jnp.zeros((total_rows,), jnp.int32).at[tree_perm].set(jnp.arang...  120 us
    psum x1, waiting for transfers between devices, shards(): leaf_grams = lax.psum(spread, ('row', 'col'))  119 us
    psum x1, blocking collectives, shards(): sample_w = lax.psum(partial_w, 'row').astype(jnp.bfloat16)  52.9 us
    another operation x49, local copies, waits for them, and re-layouts, shards(): jax.scipy.linalg.solve_triangular(factor[which], values, lower=True)  31.3 us
    all_gather x1, local copies, waits for them, and re-layouts, shards(): everything = lax.all_gather(sample, ('row', 'col'), axis=0, tiled=True)  22.6 us
  transfers between devices with their start and end apart: 3, of which 1 were waited for; matrix products, arithmetic and copies ran while one was open for 71% of the time, Pallas kernels for 0%

commit v1 on v0

--- a/solution.py
+++ b/solution.py
@@ -49,7 +49,7 @@
     chosen = stored_leaf[None, :] == leaf_range[:, None]
     masked = jnp.where(chosen[:, :, None], sample[None, :, :], jnp.zeros((), jnp.bfloat16))
     spread = jnp.einsum("lrs,rt->lst", masked, sample, preferred_element_type=jnp.float32)
-    leaf_grams = lax.psum(spread, ("row", "col"))
+    leaf_grams = lax.psum(lax.psum(spread, "row"), "col")
     for level in range(levels):
         group = 2**level
         count = leaves // group

time: 940 us -> 1030 us (1.096)
  waiting for transfers between devices: 119 us -> 206 us
    psum x1 -> x2, waiting for transfers between devices: 119 us -> 206 us  [shards(): leaf_grams = lax.psum(lax.psum(spread, 'row'), 'col')]
  transfers between devices with their start and end apart: 3 -> 4, of which waited for: 1 -> 2; matrix products, arithmetic and copies ran while one was open for 71% -> 65% of each run, Pallas kernels for 0% -> 0%
where the time goes in v1:
time: 1030 us; the launch traced here: 1020 us
  other arithmetic  481 us (47%)
  local copies, waits for them, and re-layouts  208 us (20%)
  waiting for transfers between devices  206 us (20%)
  blocking collectives  52.9 us (5%)
  matrix products  43.3 us (4%)
  between operations  14.6 us (1%)
  starting transfers between devices  12.1 us (1%)
    another operation x28, other arithmetic, shards(): factor = jnp.linalg.cholesky(mean)  276 us
    psum x2, waiting for transfers between devices, shards(): leaf_grams = lax.psum(lax.psum(spread, 'row'), 'col')  206 us
    another operation x14, other arithmetic, shards(): jax.scipy.linalg.solve_triangular(factor[which], values, lower=True)  162 us
    scatter x1, local copies, waits for them, and re-layouts, shards(): inverse = jnp.zeros((total_rows,), jnp.int32).at[tree_perm].set(jnp.arang...  120 us
    psum x1, blocking collectives, shards(): sample_w = lax.psum(partial_w, 'row').astype(jnp.bfloat16)  52.9 us
    another operation x49, local copies, waits for them, and re-layouts, shards(): jax.scipy.linalg.solve_triangular(factor[which], values, lower=True)  31.3 us
    all_gather x1, local copies, waits for them, and re-layouts, shards(): everything = lax.all_gather(sample, ('row', 'col'), axis=0, tiled=True)  22.6 us
  transfers between devices with their start and end apart: 4, of which 2 were waited for; matrix products, arithmetic and copies ran while one was open for 65% of the time, Pallas kernels for 0%

profile of v1, /device:TPU:1, one launch (start us, length us, event | category | flops | bytes accessed | tf_op | source)
XLA Modules:
  0.0 1019.2 jit_solution(7605801211079900988)
XLA Ops:
  8.1 9.7 fusion.100
  17.8 52.9 %all-reduce.8 = bf16[2048,256]{1,0:T(8,128)(2,1)S(1)} all-reduce(f32[2048,256]{1,0:T(8,128)} %fusion.100), channel_id=1, replica_groups=mesh['row'=8,'col'=16] {'row'}, use_global_device_ids=true, to_apply=%region_4.5 | all-reduce | flops 524288 | bytes 3145728 | tf_op jit(solution)/shard_map/psum | solution.py:16
  70.7 10.1 convolution_bitcast_fusion
  81.9 120.1 %scatter_custom_fusion = s32[32768]{0:T(1024)S(1)} fusion(s32[32768]{0:T(1024)S(1)} %compare_select_fusion, s32[32768]{0:T(1024)S(1)} %iota.117, s32[]{:T(128)} %copy.140), kind=kCustom, calls=%fused_computation.181 | custom fusion | bytes 131076 | tf_op jit(solution)/shard_map/scatter | solution.py:32
  203.1 4.5 fusion
  207.7 106.7 %all-reduce.5.cloned.1.call-done = f32[32,256,256]{2,1,0:T(8,128)} async-done(((f32[32,256,256]{2,1,0:T(8,128)}), f32[32,256,256]{2,1,0:T(8,128)}) %all-reduce.5.cloned.1.call-update) | async-done | bytes 8388624 | tf_op jit(solution)/shard_map/psum | solution.py:52
  314.4 12.0 %all-gather.2.cloned.1.call-start = ((), (), s32[]{:S(2)}) async-start(), calls=%async_computation.4 | async-start | bytes 16908288 | tf_op jit(solution)/shard_map/all_gather | solution.py:35
  359.9 99.6 %all-reduce.7.cloned.1.call-done = f32[32,256,256]{2,1,0:T(8,128)} async-done(((f32[32,256,256]{2,1,0:T(8,128)}), f32[32,256,256]{2,1,0:T(8,128)}) %all-reduce.7.cloned.1.call-update) | async-done | bytes 8388624 | tf_op jit(solution)/shard_map/psum | solution.py:52
  459.5 4.2 bitcast_reduce_fusion.1
  464.5 6.5 bitcast_reduce_fusion.2
  487.3 23.5 %custom-call.29 = f32[2,128,128]{2,1,0:T(8,128)S(1)} custom-call(f32[2,128,128]{2,1,0:T(8,128)S(1)} %cholesky.350), custom_call_target="Cholesky" | custom-call | tf_op jit(solution)/shard_map/jit(cholesky)/cholesky | solution.py:73
  511.1 23.5 %custom-call.39 = f32[2,128,128]{2,1,0:T(8,128)S(1)} custom-call(f32[2,128,128]{2,1,0:T(8,128)S(1)} %cholesky.356), custom_call_target="Cholesky" | custom-call | tf_op jit(solution)/shard_map/jit(cholesky)/cholesky | solution.py:73
  535.6 23.5 %custom-call.34 = f32[2,128,128]{2,1,0:T(8,128)S(1)} custom-call(f32[2,128,128]{2,1,0:T(8,128)S(1)} %cholesky.353), custom_call_target="Cholesky" | custom-call | tf_op jit(solution)/shard_map/jit(cholesky)/cholesky | solution.py:73
  559.4 23.9 %custom-call.44 = f32[2,128,128]{2,1,0:T(8,128)S(1)} custom-call(f32[2,128,128]{2,1,0:T(8,128)S(1)} %cholesky.359), custom_call_target="Cholesky" | custom-call | tf_op jit(solution)/shard_map/jit(cholesky)/cholesky | solution.py:73
  584.8 19.7 %custom-call.30 = f32[2,1,128,128]{2,3,1,0:T(8,128)S(1)} custom-call(f32[2,1,128,128]{3,2,1,0:T(8,128)S(1)} %get-tuple-element.180), custom_call_target="InvertDiagBlocksLowerTriangular" | custom-call | tf_op jit(solution)/shard_map/jit(cholesky)/cholesky | solution.py:73
  605.1 23.5 %custom-call.31 = f32[2,128,128]{2,1,0:T(8,128)S(1)} custom-call(f32[2,128,128]{2,1,0:T(8,128)S(1)} %convolution_subtract_fusion.11), custom_call_target="Cholesky" | custom-call | tf_op jit(solution)/shard_map/jit(cholesky)/cholesky | solution.py:73
  628.6 19.8 %custom-call.35 = f32[2,1,128,128]{2,3,1,0:T(8,128)S(1)} custom-call(f32[2,1,128,128]{3,2,1,0:T(8,128)S(1)} %get-tuple-element.178), custom_call_target="InvertDiagBlocksLowerTriangular" | custom-call | tf_op jit(solution)/shard_map/jit(cholesky)/cholesky | solution.py:73
  651.0 23.5 %custom-call.36 = f32[2,128,128]{2,1,0:T(8,128)S(1)} custom-call(f32[2,128,128]{2,1,0:T(8,128)S(1)} %convolution_subtract_fusion.10), custom_call_target="Cholesky" | custom-call | tf_op jit(solution)/shard_map/jit(cholesky)/cholesky | solution.py:73
  674.5 21.1 %custom-call.40 = f32[2,1,128,128]{2,3,1,0:T(8,128)} custom-call(f32[2,1,128,128]{3,2,1,0:T(8,128)} %get-tuple-element.177), custom_call_target="InvertDiagBlocksLowerTriangular" | custom-call | tf_op jit(solution)/shard_map/jit(cholesky)/cholesky | solution.py:73
  697.8 25.1 %custom-call.41 = f32[2,128,128]{2,1,0:T(8,128)} custom-call(f32[2,128,128]{2,1,0:T(8,128)} %convolution_subtract_fusion.9), custom_call_target="Cholesky" | custom-call | tf_op jit(solution)/shard_map/jit(cholesky)/cholesky | solution.py:73
  723.8 21.1 %custom-call.45 = f32[2,1,128,128]{2,3,1,0:T(8,128)} custom-call(f32[2,1,128,128]{3,2,1,0:T(8,128)} %get-tuple-element.179), custom_call_target="InvertDiagBlocksLowerTriangular" | custom-call | tf_op jit(solution)/shard_map/jit(cholesky)/cholesky | solution.py:73
  747.2 24.3 %custom-call.46 = f32[2,128,128]{2,1,0:T(8,128)S(1)} custom-call(f32[2,128,128]{2,1,0:T(8,128)} %convolution_subtract_fusion.8), custom_call_target="Cholesky" | custom-call | tf_op jit(solution)/shard_map/jit(cholesky)/cholesky | solution.py:73
  779.6 20.1 %custom-call.48 = f32[2,128,128]{1,2,0:T(8,128)S(1)} custom-call(f32[2,128,128]{2,1,0:T(8,128)S(1)} %get-tuple-element.64), custom_call_target="InvertDiagBlocksLowerTriangular" | custom-call | tf_op jit(solution)/shard_map/jit(_solve_triangular)/triangular_solve | solution.py:76
  803.7 20.3 %custom-call.47 = f32[2,128,128]{1,2,0:T(8,128)} custom-call(f32[2,128,128]{2,1,0:T(8,128)S(1)} %get-tuple-element.63), custom_call_target="InvertDiagBlocksLowerTriangular" | custom-call | tf_op jit(solution)/shard_map/jit(_solve_triangular)/triangular_solve | solution.py:76
  828.1 19.7 %custom-call.43 = f32[2,128,128]{1,2,0:T(8,128)S(1)} custom-call(f32[2,128,128]{2,1,0:T(8,128)S(1)} %get-tuple-element.62), custom_call_target="InvertDiagBlocksLowerTriangular" | custom-call | tf_op jit(solution)/shard_map/jit(_solve_triangular)/triangular_solve | solution.py:76
  851.8 19.7 %custom-call.42 = f32[2,128,128]{1,2,0:T(8,128)S(1)} custom-call(f32[2,128,128]{2,1,0:T(8,128)S(1)} %get-tuple-element.61), custom_call_target="InvertDiagBlocksLowerTriangular" | custom-call | tf_op jit(solution)/shard_map/jit(_solve_triangular)/triangular_solve | solution.py:76
  875.4 19.7 %custom-call.38 = f32[2,128,128]{1,2,0:T(8,128)S(1)} custom-call(f32[2,128,128]{2,1,0:T(8,128)S(1)} %get-tuple-element.60), custom_call_target="InvertDiagBlocksLowerTriangular" | custom-call | tf_op jit(solution)/shard_map/jit(_solve_triangular)/triangular_solve | solution.py:76
  899.1 20.5 %custom-call.37 = f32[2,128,128]{1,2,0:T(8,128)} custom-call(f32[2,128,128]{2,1,0:T(8,128)S(1)} %get-tuple-element.59), custom_call_target="InvertDiagBlocksLowerTriangular" | custom-call | tf_op jit(solution)/shard_map/jit(_solve_triangular)/triangular_solve | solution.py:76
  923.4 20.3 %custom-call.33 = f32[2,128,128]{1,2,0:T(8,128)} custom-call(f32[2,128,128]{2,1,0:T(8,128)S(1)} %get-tuple-element.58), custom_call_target="InvertDiagBlocksLowerTriangular" | custom-call | tf_op jit(solution)/shard_map/jit(_solve_triangular)/triangular_solve | solution.py:76
  947.3 20.3 %custom-call.32 = f32[2,128,128]{1,2,0:T(8,128)} custom-call(f32[2,128,128]{2,1,0:T(8,128)S(1)} %get-tuple-element.57), custom_call_target="InvertDiagBlocksLowerTriangular" | custom-call | tf_op jit(solution)/shard_map/jit(_solve_triangular)/triangular_solve | solution.py:76
  967.6 22.6 %copy.47 = bf16[32768,256]{1,0:T(8,128)(2,1)} copy(bf16[32768,256]{0,1:T(8,128)(2,1)} %all-gather.2.cloned.1.call-done) | data formatting | bytes 33554432 | tf_op jit(solution)/shard_map/all_gather | solution.py:35
  990.2 9.0 gather_fusion.2
  (269 shorter events, 144.7 us)
Async XLA Ops:
  6.5 1.6 copy-start
  6.5 195.6 %reduce-scatter.2.cloned.1.call-start = ((), (), s32[]{:S(2)}) async-start(), calls=%async_computation.1 | async-start | bytes 4456448 | tf_op jit(solution)/shard_map/reduce_scatter | solution.py:19
  80.9 0.7 copy-start.25
  80.9 0.9 copy-start.11
  80.9 233.5 %all-reduce.5.cloned.1.call-start = ((), (), s32[]{:S(2)}) async-start(), calls=%async_computation.2 | async-start | bytes 16777216 | tf_op jit(solution)/shard_map/psum | solution.py:52
  203.1 4.5 copy-start.2
  207.7 251.8 %all-reduce.7.cloned.1.call-start = ((), (), s32[]{:S(2)}) async-start(), calls=%async_computation.3 | async-start | bytes 16777216 | tf_op jit(solution)/shard_map/psum | solution.py:52
  314.4 653.2 %all-gather.2.cloned.1.call-start = ((), (), s32[]{:S(2)}) async-start(), calls=%async_computation.4 | async-start | bytes 16908288 | tf_op jit(solution)/shard_map/all_gather | solution.py:35
  486.5 0.8 copy-start.6
  511.0 93.4 %copy-start.7 = (f32[2,256,256]{2,1,0:T(8,128)S(1)}, f32[2,256,256]{2,1,0:T(8,128)}, u32[]{:S(2)}) copy-start(f32[2,256,256]{2,1,0:T(8,128)} %copy-done.6) | copy-start | bytes 1572868
  534.8 0.8 copy-start.8
  583.2 1.5 copy-start.9
  605.1 166.3 %copy-start.10 = (f32[2,128,128]{2,1,0:T(8,128)S(1)}, f32[2,128,128]{2,1,0:T(8,128)}, u32[]{:S(2)}) copy-start(f32[2,128,128]{2,1,0:T(8,128)} %copy-done.9) | copy-start | bytes 393220
  772.5 1.0 copy-start.3
  772.5 1.0 copy-start.4
  895.1 108.1 %copy-start.13 = (f32[2,128,128]{1,2,0:T(8,128)}, f32[2,128,128]{1,2,0:T(8,128)S(1)}, u32[]{:S(2)}) copy-start(f32[2,128,128]{1,2,0:T(8,128)S(1)} %custom-call.38) | copy-start | bytes 393220
  923.4 66.9 %copy-start.5 = (f32[256,256]{1,0:T(8,128)}, f32[256,256]{1,0:T(8,128)S(1)}, u32[]{:S(2)}) copy-start(f32[256,256]{1,0:T(8,128)S(1)} %get-tuple-element.606) | copy-start | bytes 786436
  967.6 31.8 %copy-start.24 = (pred[256]{0:T(512)(128)(4,1)S(1)}, pred[256]{0:T(512)(128)(4,1)}, u32[]{:S(2)}) copy-start(pred[256]{0:T(512)(128)(4,1)} %get-tuple-element.139) | copy-start | bytes 772
  967.6 32.8 %copy-start.12 = (f32[2,128,128]{1,2,0:T(8,128)S(1)}, f32[2,128,128]{1,2,0:T(8,128)}, u32[]{:S(2)}) copy-start(f32[2,128,128]{1,2,0:T(8,128)} %custom-call.47) | copy-start | bytes 393220
  999.4 10.5 %copy-start.14 = (f32[2,128,128]{1,2,0:T(8,128)S(1)}, f32[2,128,128]{1,2,0:T(8,128)}, u32[]{:S(2)}) copy-start(f32[2,128,128]{1,2,0:T(8,128)} %custom-call.33) | copy-start | bytes 393220
  999.4 10.8 %copy-start.15 = (f32[2,128,128]{1,2,0:T(8,128)S(1)}, f32[2,128,128]{1,2,0:T(8,128)}, u32[]{:S(2)}) copy-start(f32[2,128,128]{1,2,0:T(8,128)} %custom-call.32) | copy-start | bytes 393220
  999.8 11.4 %copy-start.18 = (pred[256]{0:T(512)(128)(4,1)S(1)}, pred[256]{0:T(512)(128)(4,1)}, u32[]{:S(2)}) copy-start(pred[256]{0:T(512)(128)(4,1)} %get-tuple-element.187) | copy-start | bytes 772
  999.8 11.4 %copy-start.19 = (pred[256]{0:T(512)(128)(4,1)S(1)}, pred[256]{0:T(512)(128)(4,1)}, u32[]{:S(2)}) copy-start(pred[256]{0:T(512)(128)(4,1)} %get-tuple-element.188) | copy-start | bytes 772
  1000.4 10.8 %copy-start.16 = (pred[256]{0:T(512)(128)(4,1)S(1)}, pred[256]{0:T(512)(128)(4,1)}, u32[]{:S(2)}) copy-start(pred[256]{0:T(512)(128)(4,1)} %get-tuple-element.226) | copy-start | bytes 772
  1000.4 10.8 %copy-start.17 = (pred[256]{0:T(512)(128)(4,1)S(1)}, pred[256]{0:T(512)(128)(4,1)}, u32[]{:S(2)}) copy-start(pred[256]{0:T(512)(128)(4,1)} %get-tuple-element.227) | copy-start | bytes 772
  1001.0 10.3 %copy-start.22 = (pred[256]{0:T(512)(128)(4,1)S(1)}, pred[256]{0:T(512)(128)(4,1)}, u32[]{:S(2)}) copy-start(pred[256]{0:T(512)(128)(4,1)} %get-tuple-element.183) | copy-start | bytes 772
  1001.0 10.3 %copy-start.23 = (pred[256]{0:T(512)(128)(4,1)S(1)}, pred[256]{0:T(512)(128)(4,1)}, u32[]{:S(2)}) copy-start(pred[256]{0:T(512)(128)(4,1)} %get-tuple-element.184) | copy-start | bytes 772
  1001.6 9.7 copy-start.20
  1001.6 9.7 copy-start.21
  1003.5 9.0 copy-start.1
Sparse Core Ops, SparseCore 0:
  81.0 79.6 reduce-scatter.1
  207.8 106.5 all-reduce.4
  318.0 141.4 all-reduce.6
  462.2 99.0 all-gather.1
